TPU v7x, 32 devices: a whole 2x2x4 slice. The times are simulated.
32 devices in a mesh: dom: 16 (over z, y, x), mem: 2 (over core).
Axes of the slice: x: 2, y: 2, z: 4, core: 2. Of those that a mesh axis runs over, the one named last changes fastest.
Arguments:
- node_latents: bfloat16 [4, 2048, 512], P('mem', 'dom'), may hold values from -6 to 6
- edge_latents: bfloat16 [4, 8192, 512], P('mem', 'dom'), may hold values from -6 to 6
- edge_senders: int32 [8192], P('dom'), may hold values from 0 to 191, as said below
- edge_receivers: int32 [8192], P('dom'), may hold values from 0 to 127
- edge_counts: int32 [16], P('dom'), may hold values from 64 to 512, as said below
- halo_send: int32 [512], P('dom'), may hold values from 0 to 127
- long_send: int32 [16, 16, 2], replicated, may hold values from 0 to 3
- edge_first: bfloat16 [2, 1536, 512], P(None, None, 'mem'), may hold values from -0.15625 to 0.15625
- edge_second: bfloat16 [2, 512, 512], P(None, None, 'mem'), may hold values from -0.25 to 0.25
- node_first: bfloat16 [2, 1024, 512], P(None, None, 'mem'), may hold values from -0.1875 to 0.1875
- node_second: bfloat16 [2, 512, 512], P(None, None, 'mem'), may hold values from -0.25 to 0.25
- edge_gain: float32 [2, 512], replicated, may hold values from 0.5 to 1.5
- edge_shift: float32 [2, 512], replicated, may hold values from -3 to 3
- node_gain: float32 [2, 512], replicated, may hold values from 0.5 to 1.5
- node_shift: float32 [2, 512], replicated, may hold values from -3 to 3
Outputs:
- node_out: bfloat16 [4, 2048, 512], P('mem', 'dom')
- edge_out: bfloat16 [4, 8192, 512], P('mem', 'dom')
Inputs may be any that keep to these rules, and one draw needn't show every extreme that they name: `edge_senders`: rows below 128 are the partition's own nodes, the next 32 its neighbours' sent nodes, the rest the coarse slots of all partitions. `edge_counts`: live slots come first in each partition; some partition has exactly 512 live slots.
All inputs are finite; a program needn't handle non-finite values.
Results may differ from a plain program's by a relative error of at most 0.0075.
Values may be sent and summed in bfloat16 or wider, within the bound.
A program may use at most 128 MiB of HBM per device.

v0:
```python
import jax
import jax.numpy as jnp
from jax import lax
from jax.sharding import PartitionSpec as P

HALO = 16
LAYERS = 2


def with_halo(block, sides, width):
    for axis, dim in sides:
        count = lax.axis_size(axis)
        forward = [(i, i + 1) for i in range(count - 1)]
        forward.append((count - 1, 0))
        backward = [(target, source) for source, target in forward]
        low = lax.ppermute(
            lax.slice_in_dim(block, block.shape[dim] - width, None, axis=dim), axis, forward
        )
        high = lax.ppermute(lax.slice_in_dim(block, 0, width, axis=dim), axis, backward)
        block = jnp.concatenate([low, block, high], axis=dim)
    return block


def project_norm(inputs, first_weight, second, scale_gain, offset):
    hidden = jax.nn.silu(jnp.dot(inputs, first_weight, preferred_element_type=jnp.float32)).astype(
        jnp.bfloat16
    )
    output = jnp.dot(hidden, second, preferred_element_type=jnp.float32)
    average = jnp.mean(output, -1, keepdims=True)
    centred = output - average
    variance = jnp.mean(centred * centred, -1, keepdims=True)
    return centred * lax.rsqrt(variance + 1e-05) * scale_gain + offset


def per_device(
    node_latents,
    edge_latents,
    edge_senders,
    edge_receivers,
    edge_counts,
    halo_send,
    long_send,
    edge_first,
    edge_second,
    node_first,
    node_second,
    edge_gain,
    edge_shift,
    node_gain,
    node_shift,
):
    members, node_rows, features = node_latents.shape
    edge_rows = edge_latents.shape[1]
    position = lax.axis_index("dom")
    live_count = edge_counts[0]
    live_mask = jnp.arange(edge_rows, dtype=jnp.int32) < live_count
    onehot = (
        (edge_receivers[None, :] == jnp.arange(node_rows, dtype=jnp.int32)[:, None])
        & live_mask[None, :]
    ).astype(jnp.bfloat16)
    node_state = node_latents
    edge_state = edge_latents
    for layer_index in range(LAYERS):
        edge_inner, edge_outer, node_inner, node_outer = (
            lax.all_gather(edge_first[layer_index], "mem", axis=1, tiled=True),
            lax.all_gather(edge_second[layer_index], "mem", axis=1, tiled=True),
            lax.all_gather(node_first[layer_index], "mem", axis=1, tiled=True),
            lax.all_gather(node_second[layer_index], "mem", axis=1, tiled=True),
        )
        outgoing = jnp.take(node_state, halo_send, axis=1)
        bordered = with_halo(outgoing, (("dom", 1),), HALO)
        from_left = bordered[:, :HALO]
        from_right = bordered[:, 3 * HALO :]
        send_rows = lax.dynamic_index_in_dim(long_send, position, 0, keepdims=False).reshape(-1)
        packed = jnp.take(node_state, send_rows, axis=1)
        far_rows = lax.all_to_all(packed, "dom", split_axis=1, concat_axis=1, tiled=True)
        sources = jnp.concatenate([node_state, from_left, from_right, far_rows], 1)
        sender_rows = jnp.take(sources, edge_senders, axis=1)
        receiver_rows = jnp.take(node_state, edge_receivers, axis=1)
        joined = jnp.concatenate([edge_state, sender_rows, receiver_rows], -1)
        update = project_norm(
            joined.reshape(members * edge_rows, 3 * features),
            edge_inner,
            edge_outer,
            edge_gain[layer_index],
            edge_shift[layer_index],
        ).reshape(members, edge_rows, features)
        new_edges = jnp.where(
            live_mask[None, :, None], edge_state.astype(jnp.float32) + update, 0.0
        ).astype(jnp.bfloat16)
        summed = jnp.einsum(
            "ne,med->mnd", onehot, new_edges, preferred_element_type=jnp.float32
        ).astype(jnp.bfloat16)
        node_in = jnp.concatenate([node_state, summed], -1).reshape(
            members * node_rows, 2 * features
        )
        node_update = project_norm(
            node_in, node_inner, node_outer, node_gain[layer_index], node_shift[layer_index]
        ).reshape(members, node_rows, features)
        node_state = (node_state.astype(jnp.float32) + node_update).astype(jnp.bfloat16)
        edge_state = new_edges
    return (node_state, edge_state)


def solution(mesh):
    placed = (
        P("mem", "dom", None),
        P("mem", "dom", None),
        P("dom"),
        P("dom"),
        P("dom"),
        P("dom"),
        P(),
        P(None, None, "mem"),
        P(None, None, "mem"),
        P(None, None, "mem"),
        P(None, None, "mem"),
        P(),
        P(),
        P(),
        P(),
    )
    return jax.shard_map(
        per_device,
        mesh=mesh,
        in_specs=placed,
        out_specs=(P("mem", "dom", None), P("mem", "dom", None)),
        check_vma=False,
    )
```

profile of v0, /device:TPU:0, one launch (start us, length us, event | category | flops | bytes accessed | tf_op | source)
XLA Modules:
  0.0 136.8 jit_solution(4153508605069682487)
XLA Ops:
  7.2 2.7 %fusion.60 = (bf16[1,1536,256]{2,1,0:T(8,128)(2,1)}, bf16[1,1536,256]{2,1,0:T(8,128)(2,1)}) fusion(bf16[2,1536,256]{2,1,0:T(8,128)(2,1)} %param.28), kind=kLoop, calls=%fused_computation.105 | loop fusion | bytes 3145728 | tf_op jit(solution)/shard_map/slice | solution.py:65
  13.7 8.3 %all-to-all-start = ((bf16[2,32,512]{2,0,1:T(2,128)(2,1)}), bf16[2,32,512]{2,0,1:T(2,128)(2,1)S(1)}, u32[]{:S(2)}, u32[]{:S(2)}) async-start(bf16[2,32,512]{2,0,1:T(2,128)(2,1)} %copy.84), calls=%async_computation | async-start | bytes 131072 | tf_op jit(solution)/shard_map/all_to_all | solution.py:76
  25.0 3.7 %collective-permute-start.1 = (bf16[2,16,512]{2,1,0:T(8,128)(2,1)S(1)}, bf16[2,16,512]{2,1,0:T(8,128)(2,1)S(1)}, u32[]{:S(2)}, u32[]{:S(2)}) collective-permute-start(bf16[2,16,512]{2,1,0:T(8,128)(2,1)S(1)} %get-tuple-element.24), channel_id=1, source_target_pairs={{2,0},{4,2},{6,4},{8,6},{10,8},{12,10},{14,12},{16,14},{18,16},{20... | collective-permute-start | bytes 98312 | tf_op jit(solution)/shard_map/ppermute | solution.py:19
  28.9 4.4 %gather_fusion.3 = bf16[512,2,512]{2,0,1:T(8,128)(2,1)S(1)} fusion(bf16[2,128,512]{2,1,0:T(8,128)(2,1)S(1)} %copy-done.1, s32[1024]{0:T(1024)S(1)} %pad_clamp_fusion), kind=kCustom, calls=%fused_computation.2.clone | custom fusion | bytes 2099200 | tf_op jit(solution)/shard_map/jit(_take)/gather | solution.py:79
  33.4 2.4 %all-gather.1 = bf16[1,512,512]{2,1,0:T(8,128)(2,1)} all-gather(bf16[1,512,256]{2,1,0:T(8,128)(2,1)S(1)} %get-tuple-element.18), channel_id=3, replica_groups=mesh['dom'=16,'mem'=2] {'mem'}, dimensions={2}, use_global_device_ids=true | all-gather | bytes 786432 | tf_op jit(solution)/shard_map/all_gather | solution.py:66
  35.9 2.3 %all-gather.3 = bf16[1,512,512]{2,1,0:T(8,128)(2,1)} all-gather(bf16[1,512,256]{2,1,0:T(8,128)(2,1)S(1)} %get-tuple-element.19), channel_id=5, replica_groups=mesh['dom'=16,'mem'=2] {'mem'}, dimensions={2}, use_global_device_ids=true | all-gather | bytes 786432 | tf_op jit(solution)/shard_map/all_gather | solution.py:68
  38.3 2.3 %all-gather.5 = bf16[1,512,512]{2,1,0:T(8,128)(2,1)} all-gather(bf16[1,512,256]{2,1,0:T(8,128)(2,1)S(1)} %get-tuple-element.17), channel_id=7, replica_groups=mesh['dom'=16,'mem'=2] {'mem'}, dimensions={2}, use_global_device_ids=true | all-gather | bytes 786432 | tf_op jit(solution)/shard_map/all_gather | solution.py:66
  40.6 2.6 %all-gather.7 = bf16[1,512,512]{2,1,0:T(8,128)(2,1)} all-gather(bf16[1,512,256]{2,1,0:T(8,128)(2,1)S(1)} %get-tuple-element.20), channel_id=9, replica_groups=mesh['dom'=16,'mem'=2] {'mem'}, dimensions={2}, use_global_device_ids=true | all-gather | bytes 786432 | tf_op jit(solution)/shard_map/all_gather | solution.py:68
  43.2 5.0 %fusion.29 = bf16[2,512,512]{2,0,1:T(2,128)(2,1)} fusion(bf16[512,2,512]{2,0,1:T(8,128)(2,1)S(1)} %gather_fusion.3, pred[512]{0:T(512)(128)(4,1)S(1)} %compare_and_fusion), kind=kLoop, calls=%fused_computation.45 | loop fusion | flops 524288 | bytes 2097664 | tf_op jit(solution)/shard_map/jit(_take)/select_n | solution.py:79
  52.1 3.6 %gather_fusion.2 = bf16[512,2,512]{2,1,0:T(2,128)(2,1)S(1)} fusion(bf16[2,192,512]{2,0,1:T(2,128)(2,1)S(1)} %pad_maximum_fusion.5, s32[1024]{0:T(1024)S(1)} %pad_clamp_fusion.1), kind=kCustom, calls=%fused_computation.1.clone | custom fusion | bytes 2099200 | tf_op jit(solution)/shard_map/jit(_take)/gather | solution.py:78
  57.7 3.3 %pad_maximum_fusion = bf16[2,512,1536]{2,0,1:T(2,128)(2,1)S(1)} fusion(bf16[2,512,512]{2,0,1:T(2,128)(2,1)S(1)} %copy-done.4, bf16[2,512,512]{2,0,1:T(2,128)(2,1)S(1)} %fusion.27, bf16[2,512,512]{2,0,1:T(2,128)(2,1)S(1)} %copy-done.6), kind=kLoop, calls=%fused_computation.8 | loop fusion | flops 9437184 | bytes 6291456 | tf_op jit(solution)/shard_map/concatenate | solution.py:80
  61.0 2.1 %copy.90 = bf16[2,512,1536]{2,1,0:T(8,128)(2,1)} copy(bf16[2,512,1536]{2,0,1:T(2,128)(2,1)S(1)} %pad_maximum_fusion) | data formatting | bytes 6291456 | tf_op jit(solution)/shard_map/concatenate | solution.py:80
  63.1 5.0 %fusion.70 = (f32[1024]{0:T(1024)S(1)}, f32[1024,512]{1,0:T(8,128)S(1)}) fusion(bf16[1,512,512]{2,1,0:T(8,128)(2,1)} %all-gather.1, bf16[1024,1536]{1,0:T(8,128)(2,1)} %bitcast.105, bf16[1,1536,512]{2,1,0:T(8,128)(2,1)} %all-gather.13.cloned.1.call-done), kind=kOutput, calls=%fused_computation.115 | convolution fusion | flops 2150628352 | bytes 7344128 | tf_op jit(solution)/shard_map/dot_general | solution.py:28
  68.9 5.5 %fusion.3 = bf16[2,512,512]{2,0,1:T(2,128)(2,1)S(1)} fusion(f32[2,512,512]{2,1,0:T(8,128)S(1)} %bitcast.104, pred[512]{0:T(512)(128)(4,1)S(1)} %iota_compare_fusion.1, bf16[2,512,512]{2,1,0:T(8,128)(2,1)S(1)} %copy-done.2), kind=kLoop, calls=%fused_computation.15 | loop fusion | flops 2097152 | bytes 4194816 | tf_op jit(solution)/shard_map/convert_element_type | solution.py:90
  80.1 3.6 %gather_fusion.7 = bf16[512,2,512]{2,1,0:T(2,128)(2,1)S(1)} fusion(bf16[2,128,512]{2,0,1:T(2,128)(2,1)S(1)} %copy.96, s32[1024]{0:T(1024)S(1)} %pad_clamp_fusion), kind=kCustom, calls=%fused_computation.7.clone | custom fusion | bytes 2099200 | tf_op jit(solution)/shard_map/jit(_take)/gather | solution.py:79
  84.7 5.6 %collective-permute-start.3 = (bf16[2,16,512]{1,2,0:T(8,128)(2,1)S(1)}, bf16[2,16,512]{1,2,0:T(8,128)(2,1)}, u32[]{:S(2)}, u32[]{:S(2)}) collective-permute-start(bf16[2,16,512]{1,2,0:T(8,128)(2,1)S(1)} %get-tuple-element.22), channel_id=1, source_target_pairs={{2,0},{4,2},{6,4},{8,6},{10,8},{12,10},{14,12},{16,14},{18,16},{20... | collective-permute-start | bytes 98312 | tf_op jit(solution)/shard_map/ppermute | solution.py:19
  91.1 3.5 %all-to-all-start.1 = ((bf16[2,32,512]{2,0,1:T(2,128)(2,1)}), bf16[2,32,512]{2,0,1:T(2,128)(2,1)S(1)}, u32[]{:S(2)}, u32[]{:S(2)}) async-start(bf16[2,32,512]{2,0,1:T(2,128)(2,1)} %fusion.55), calls=%async_computation.1 | async-start | bytes 131072 | tf_op jit(solution)/shard_map/all_to_all | solution.py:76
  94.6 2.6 %fusion.30 = bf16[2,512,512]{2,0,1:T(2,128)(2,1)} fusion(bf16[512,2,512]{2,1,0:T(2,128)(2,1)S(1)} %gather_fusion.7, pred[512]{0:T(512)(128)(4,1)S(1)} %compare_and_fusion), kind=kLoop, calls=%fused_computation.46 | loop fusion | flops 524288 | bytes 2097664 | tf_op jit(solution)/shard_map/jit(_take)/select_n | solution.py:79
  97.2 4.9 %all-to-all-done.1 = bf16[2,32,512]{2,0,1:T(2,128)(2,1)S(1)} async-done(((bf16[2,32,512]{2,0,1:T(2,128)(2,1)}), bf16[2,32,512]{2,0,1:T(2,128)(2,1)S(1)}, u32[]{:S(2)}, u32[]{:S(2)}) %all-to-all-start.1) | async-done | bytes 65568 | tf_op jit(solution)/shard_map/all_to_all | solution.py:76
  104.0 3.6 %gather_fusion.6 = bf16[512,2,512]{2,1,0:T(2,128)(2,1)S(1)} fusion(bf16[2,192,512]{2,0,1:T(2,128)(2,1)S(1)} %copy.100, s32[1024]{0:T(1024)S(1)} %pad_clamp_fusion.1), kind=kCustom, calls=%fused_computation.6.clone | custom fusion | bytes 2099200 | tf_op jit(solution)/shard_map/jit(_take)/gather | solution.py:78
  109.6 3.3 %pad_maximum_fusion.1 = bf16[2,512,1536]{2,0,1:T(2,128)(2,1)S(1)} fusion(bf16[2,512,512]{2,0,1:T(2,128)(2,1)S(1)} %copy-done.5, bf16[2,512,512]{2,0,1:T(2,128)(2,1)S(1)} %fusion.28, bf16[2,512,512]{2,0,1:T(2,128)(2,1)S(1)} %fusion.3), kind=kLoop, calls=%fused_computation.9 | loop fusion | flops 9437184 | bytes 6291456 | tf_op jit(solution)/shard_map/concatenate | solution.py:80
  112.9 2.1 %copy.102 = bf16[2,512,1536]{2,1,0:T(8,128)(2,1)} copy(bf16[2,512,1536]{2,0,1:T(2,128)(2,1)S(1)} %pad_maximum_fusion.1) | data formatting | bytes 6291456 | tf_op jit(solution)/shard_map/concatenate | solution.py:80
  115.0 5.0 %fusion.76 = (f32[1024]{0:T(1024)S(1)}, f32[1024,512]{1,0:T(8,128)S(1)}) fusion(bf16[1,512,512]{2,1,0:T(8,128)(2,1)} %all-gather.5, bf16[1024,1536]{1,0:T(8,128)(2,1)} %bitcast.106, bf16[1,1536,512]{2,1,0:T(8,128)(2,1)} %all-gather.17.cloned.1.call-done), kind=kOutput, calls=%fused_computation.117 | convolution fusion | flops 2150628352 | bytes 7344128 | tf_op jit(solution)/shard_map/dot_general | solution.py:28
  120.8 4.3 %fusion.1 = bf16[2,512,512]{2,0,1:T(2,128)(2,1)S(1)} fusion(f32[2,512,512]{2,1,0:T(8,128)S(1)} %bitcast.103, bf16[2,512,512]{2,0,1:T(2,128)(2,1)S(1)} %fusion.3, pred[512]{0:T(512)(128)(4,1)S(1)} %iota_compare_fusion.1), kind=kLoop, calls=%fused_computation.12 | loop fusion | flops 2097152 | bytes 4194816 | tf_op jit(solution)/shard_map/convert_element_type | solution.py:90
  (138 shorter events, 29.8 us)
Async XLA Ops:
  7.2 4.8 %copy-start = (s32[16,16,2]{1,2,0:T(2,128)S(1)}, s32[16,16,2]{1,2,0:T(2,128)}, u32[]{:S(2)}) copy-start(s32[16,16,2]{1,2,0:T(2,128)} %param.27) | copy-start | bytes 6148
  7.2 2.9 %copy-start.9 = (bf16[2,1024,256]{2,1,0:T(8,128)(2,1)S(1)}, bf16[2,1024,256]{2,1,0:T(8,128)(2,1)}, u32[]{:S(2)}) copy-start(bf16[2,1024,256]{2,1,0:T(8,128)(2,1)} %param.30) | copy-start | bytes 3145732
  7.2 55.9 %all-gather.13.cloned.1.call-start = ((), (), s32[]{:S(2)}) async-start(), calls=%async_computation.2 | async-start | bytes 2359296 | tf_op jit(solution)/shard_map/all_gather | solution.py:65
  10.0 12.1 %copy-start.20 = (s32[32]{0:T(128)S(1)}, s32[32]{0:T(128)}, u32[]{:S(2)}) copy-start(s32[32]{0:T(128)} %param.26) | copy-start | bytes 388
  10.0 65.2 %all-gather.15.cloned.1.call-start = ((), (), s32[]{:S(2)}) async-start(), calls=%async_computation.3 | async-start | bytes 1572864 | tf_op jit(solution)/shard_map/all_gather | solution.py:67
  11.2 17.6 %copy-start.15 = (s32[512]{0:T(512)S(1)}, s32[512]{0:T(512)}, u32[]{:S(2)}) copy-start(s32[512]{0:T(512)} %param.23) | copy-start | bytes 6148
  11.2 17.6 %copy-start.14 = (s32[512]{0:T(512)S(1)}, s32[512]{0:T(512)}, u32[]{:S(2)}) copy-start(s32[512]{0:T(512)} %param.24) | copy-start | bytes 6148
  11.2 103.8 %all-gather.17.cloned.1.call-start = ((), (), s32[]{:S(2)}) async-start(), calls=%async_computation.4 | async-start | bytes 2359296 | tf_op jit(solution)/shard_map/all_gather | solution.py:65
  13.7 37.8 %all-to-all-start = ((bf16[2,32,512]{2,0,1:T(2,128)(2,1)}), bf16[2,32,512]{2,0,1:T(2,128)(2,1)S(1)}, u32[]{:S(2)}, u32[]{:S(2)}) async-start(bf16[2,32,512]{2,0,1:T(2,128)(2,1)} %copy.84), calls=%async_computation | async-start | bytes 131072 | tf_op jit(solution)/shard_map/all_to_all | solution.py:76
  22.1 104.0 %all-gather.19.cloned.1.call-start = ((), (), s32[]{:S(2)}) async-start(), calls=%async_computation.5 | async-start | bytes 1572864 | tf_op jit(solution)/shard_map/all_gather | solution.py:67
  23.0 28.3 %collective-permute-start = (bf16[2,16,512]{2,1,0:T(8,128)(2,1)S(1)}, bf16[2,16,512]{2,1,0:T(8,128)(2,1)S(1)}, u32[]{:S(2)}, u32[]{:S(2)}) collective-permute-start(bf16[2,16,512]{2,1,0:T(8,128)(2,1)S(1)} %get-tuple-element.23), channel_id=1, source_target_pairs={{0,2},{2,4},{4,6},{6,8},{8,10},{10,12},{12,14},{14,16},{16,18},{18... | collective-permute-start | bytes 98312 | tf_op jit(solution)/shard_map/ppermute | solution.py:16
  25.0 26.4 %collective-permute-start.1 = (bf16[2,16,512]{2,1,0:T(8,128)(2,1)S(1)}, bf16[2,16,512]{2,1,0:T(8,128)(2,1)S(1)}, u32[]{:S(2)}, u32[]{:S(2)}) collective-permute-start(bf16[2,16,512]{2,1,0:T(8,128)(2,1)S(1)} %get-tuple-element.24), channel_id=1, source_target_pairs={{2,0},{4,2},{6,4},{8,6},{10,8},{12,10},{14,12},{16,14},{18,16},{20... | collective-permute-start | bytes 98312 | tf_op jit(solution)/shard_map/ppermute | solution.py:19
  28.8 4.5 %copy-start.12 = (bf16[2,512,256]{2,1,0:T(8,128)(2,1)S(1)}, bf16[2,512,256]{2,1,0:T(8,128)(2,1)}, u32[]{:S(2)}) copy-start(bf16[2,512,256]{2,1,0:T(8,128)(2,1)} %param.29) | copy-start | bytes 1572868
  28.8 7.0 %copy-start.16 = (f32[2,512]{1,0:T(2,128)S(1)}, f32[2,512]{1,0:T(2,128)}, u32[]{:S(2)}) copy-start(f32[2,512]{1,0:T(2,128)} %param.32) | copy-start | bytes 12292
  28.8 7.0 %copy-start.17 = (f32[2,512]{1,0:T(2,128)S(1)}, f32[2,512]{1,0:T(2,128)}, u32[]{:S(2)}) copy-start(f32[2,512]{1,0:T(2,128)} %param.33) | copy-start | bytes 12292
  33.3 2.6 %copy-start.13 = (bf16[2,512,256]{2,1,0:T(8,128)(2,1)S(1)}, bf16[2,512,256]{2,1,0:T(8,128)(2,1)}, u32[]{:S(2)}) copy-start(bf16[2,512,256]{2,1,0:T(8,128)(2,1)} %param.31) | copy-start | bytes 1572868
  33.3 4.9 %copy-start.18 = (f32[2,512]{1,0:T(2,128)S(1)}, f32[2,512]{1,0:T(2,128)}, u32[]{:S(2)}) copy-start(f32[2,512]{1,0:T(2,128)} %param.34) | copy-start | bytes 12292
  33.3 4.9 %copy-start.19 = (f32[2,512]{1,0:T(2,128)S(1)}, f32[2,512]{1,0:T(2,128)}, u32[]{:S(2)}) copy-start(f32[2,512]{1,0:T(2,128)} %param.35) | copy-start | bytes 12292
  40.6 8.7 %copy-start.2 = (bf16[2,512,512]{2,1,0:T(8,128)(2,1)S(1)}, bf16[2,512,512]{2,1,0:T(8,128)(2,1)}, u32[]{:S(2)}) copy-start(bf16[2,512,512]{2,1,0:T(8,128)(2,1)} %param.22) | copy-start | bytes 3145732
  49.3 25.6 %copy-start.7 = (bf16[2,128,512]{1,2,0:T(8,128)(2,1)}, bf16[2,128,512]{1,2,0:T(8,128)(2,1)S(1)}, u32[]{:S(2)}) copy-start(bf16[2,128,512]{1,2,0:T(8,128)(2,1)S(1)} %copy.81) | copy-start | bytes 786436
  84.7 17.6 %collective-permute-start.2 = (bf16[2,16,512]{1,2,0:T(8,128)(2,1)}, bf16[2,16,512]{1,2,0:T(8,128)(2,1)S(1)}, u32[]{:S(2)}, u32[]{:S(2)}) collective-permute-start(bf16[2,16,512]{1,2,0:T(8,128)(2,1)} %get-tuple-element.21), channel_id=1, source_target_pairs={{0,2},{2,4},{4,6},{6,8},{8,10},{10,12},{12,14},{14,16},{16,18},{18... | collective-permute-start | bytes 98312 | tf_op jit(solution)/shard_map/ppermute | solution.py:16
  84.7 17.6 %collective-permute-start.3 = (bf16[2,16,512]{1,2,0:T(8,128)(2,1)S(1)}, bf16[2,16,512]{1,2,0:T(8,128)(2,1)}, u32[]{:S(2)}, u32[]{:S(2)}) collective-permute-start(bf16[2,16,512]{1,2,0:T(8,128)(2,1)S(1)} %get-tuple-element.22), channel_id=1, source_target_pairs={{2,0},{4,2},{6,4},{8,6},{10,8},{12,10},{14,12},{16,14},{18,16},{20... | collective-permute-start | bytes 98312 | tf_op jit(solution)/shard_map/ppermute | solution.py:19
  91.1 11.0 %all-to-all-start.1 = ((bf16[2,32,512]{2,0,1:T(2,128)(2,1)}), bf16[2,32,512]{2,0,1:T(2,128)(2,1)S(1)}, u32[]{:S(2)}, u32[]{:S(2)}) async-start(bf16[2,32,512]{2,0,1:T(2,128)(2,1)} %fusion.55), calls=%async_computation.1 | async-start | bytes 131072 | tf_op jit(solution)/shard_map/all_to_all | solution.py:76
  125.3 3.4 %copy-start.3 = (bf16[2,512,512]{2,1,0:T(8,128)(2,1)}, bf16[2,512,512]{2,1,0:T(8,128)(2,1)S(1)}, u32[]{:S(2)}) copy-start(bf16[2,512,512]{2,1,0:T(8,128)(2,1)S(1)} %copy.108) | copy-start | bytes 3145732
  (7 other events, 11.6 us)
Sparse Core Ops, SparseCore 0:
  10.1 12.1 all-gather.12
  23.9 9.9 all-gather.14
  35.4 10.6 all-gather.16
  47.5 9.9 all-gather.18
where the time goes:
time: 137 us
  local copies, waits for them, and re-layouts  34.7 us (25%)
  other arithmetic  33.2 us (24%)
  starting transfers between devices  23.3 us (17%)
  between operations  15.2 us (11%)
  matrix products  15.1 us (11%)
  blocking collectives  9.69 us (7%)
  waiting for transfers between devices  5.66 us (4%)
    dot_general x4, matrix products, project_norm(): output = jnp.dot(hidden, second, preferred_element_type=jnp.float32)  14.1 us
    all_to_all x2, starting transfers between devices, per_device(): lax.all_to_all(packed, 'dom', split_axis=1, concat_axis=1, tiled=True)  11.8 us
    convert_element_type x2, other arithmetic, per_device(): new_edges = jnp.where(live_mask[None, :, None], edge_state.astype(jnp.flo...  9.73 us
    ppermute x2, starting transfers between devices, with_halo(): lax.ppermute(lax.slice_in_dim(block, 0, width, axis=dim), axis, backward)  9.32 us
    gather x2, local copies, waits for them, and re-layouts, per_device(): receiver_rows = jnp.take(node_state, edge_receivers, axis=1)  8 us
    select_n x3, other arithmetic, per_device(): receiver_rows = jnp.take(node_state, edge_receivers, axis=1)  7.59 us
    gather x2, local copies, waits for them, and re-layouts, per_device(): sender_rows = jnp.take(sources, edge_senders, axis=1)  7.11 us
    concatenate x2, other arithmetic, per_device(): joined = jnp.concatenate([edge_state, sender_rows, receiver_rows], -1)  6.59 us
  transfers between devices with their start and end apart: 10, of which 1 were waited for; matrix products, arithmetic and copies ran while one was open for 55% of the time, Pallas kernels for 0%

commit v1 on v0

--- a/solution.py
+++ b/solution.py
@@ -73,7 +73,10 @@
         from_right = bordered[:, 3 * HALO :]
         send_rows = lax.dynamic_index_in_dim(long_send, position, 0, keepdims=False).reshape(-1)
         packed = jnp.take(node_state, send_rows, axis=1)
-        far_rows = lax.all_to_all(packed, "dom", split_axis=1, concat_axis=1, tiled=True)
+        far_rows = jnp.concatenate(
+            lax.all_to_all(jnp.stack(jnp.split(packed, lax.axis_size("dom"), axis=1)), "dom", 0, 0),
+            axis=1,
+        )
         sources = jnp.concatenate([node_state, from_left, from_right, far_rows], 1)
         sender_rows = jnp.take(sources, edge_senders, axis=1)
         receiver_rows = jnp.take(node_state, edge_receivers, axis=1)

time: 137 us -> 157 us (1.15)
  local copies, waits for them, and re-layouts: 34.7 us -> 53 us
  waiting for transfers between devices: 5.66 us -> 7.72 us
    unnamed x46 -> x76, local copies, waits for them, and re-layouts: 4.66 us -> 22.4 us
    ppermute x2, waiting for transfers between devices: 0.01 us -> 5.02 us  [with_halo(): lax.ppermute(lax.slice_in_dim(block, block.shape[dim] - width, None, axis...]
    all_to_all x2, waiting for transfers between devices: 4.88 us -> 0.01 us  [per_device(): lax.all_to_all(jnp.stack(jnp.split(packed, lax.axis_size('dom'), axis=1))...]
    ppermute x2, starting transfers between devices: 9.32 us -> 7.4 us  [with_halo(): lax.ppermute(lax.slice_in_dim(block, 0, width, axis=dim), axis, backward)]
    ppermute x2, starting transfers between devices: 1.98 us -> 3.9 us  [with_halo(): lax.ppermute(lax.slice_in_dim(block, block.shape[dim] - width, None, axis...]
    ppermute x2, waiting for transfers between devices: 0.01 us -> 1.92 us  [with_halo(): lax.ppermute(lax.slice_in_dim(block, 0, width, axis=dim), axis, backward)]
  transfers between devices with their start and end apart: 10 -> 10, of which waited for: 1 -> 2; matrix products, arithmetic and copies ran while one was open for 55% -> 59% of each run, Pallas kernels for 0% -> 0%
where the time goes in v1:
time: 157 us
  local copies, waits for them, and re-layouts  53 us (34%)
  other arithmetic  32.5 us (21%)
  starting transfers between devices  23.5 us (15%)
  between operations  15.2 us (10%)
  matrix products  15.1 us (10%)
  blocking collectives  9.69 us (6%)
  waiting for transfers between devices  7.72 us (5%)
    unnamed x76, local copies, waits for them, and re-layouts  22.4 us
    dot_general x4, matrix products, project_norm(): output = jnp.dot(hidden, second, preferred_element_type=jnp.float32)  14.1 us
    all_to_all x2, starting transfers between devices, per_device(): lax.all_to_all(jnp.stack(jnp.split(packed, lax.axis_size('dom'), axis=1))...  12 us
    convert_element_type x2, other arithmetic, per_device(): new_edges = jnp.where(live_mask[None, :, None], edge_state.astype(jnp.flo...  9.73 us
    gather x2, local copies, waits for them, and re-layouts, per_device(): receiver_rows = jnp.take(node_state, edge_receivers, axis=1)  8 us
    select_n x3, other arithmetic, per_device(): receiver_rows = jnp.take(node_state, edge_receivers, axis=1)  7.56 us
    ppermute x2, starting transfers between devices, with_halo(): lax.ppermute(lax.slice_in_dim(block, 0, width, axis=dim), axis, backward)  7.4 us
    gather x2, local copies, waits for them, and re-layouts, per_device(): sender_rows = jnp.take(sources, edge_senders, axis=1)  7.11 us
  transfers between devices with their start and end apart: 10, of which 2 were waited for; matrix products, arithmetic and copies ran while one was open for 59% of the time, Pallas kernels for 0%

profile of v1, /device:TPU:0, one launch (start us, length us, event | category | flops | bytes accessed | tf_op | source)
XLA Modules:
  0.0 156.7 jit_solution(93415451599617697)
XLA Ops:
  7.2 2.7 %fusion.60 = (bf16[1,1536,256]{2,1,0:T(8,128)(2,1)}, bf16[1,1536,256]{2,1,0:T(8,128)(2,1)}) fusion(bf16[2,1536,256]{2,1,0:T(8,128)(2,1)} %param.28), kind=kLoop, calls=%fused_computation.169 | loop fusion | bytes 3145728 | tf_op jit(solution)/shard_map/slice | solution.py:65
  22.6 8.3 %all-to-all-start = ((bf16[16,2,2,512]{3,2,1,0:T(2,128)(2,1)}), bf16[16,2,2,512]{3,2,1,0:T(2,128)(2,1)S(1)}, u32[]{:S(2)}, u32[]{:S(2)}) async-start(bf16[16,2,2,512]{3,2,1,0:T(2,128)(2,1)} %constant_dynamic-update-slice_fusion), calls=%async_computation | async-start | bytes 131072 | tf_op jit(solution)/shard_map/all_to_all | solution.py:77
  33.9 3.7 %collective-permute-start.1 = (bf16[2,16,512]{2,1,0:T(8,128)(2,1)S(1)}, bf16[2,16,512]{2,1,0:T(8,128)(2,1)S(1)}, u32[]{:S(2)}, u32[]{:S(2)}) collective-permute-start(bf16[2,16,512]{2,1,0:T(8,128)(2,1)S(1)} %get-tuple-element.22), channel_id=1, source_target_pairs={{2,0},{4,2},{6,4},{8,6},{10,8},{12,10},{14,12},{16,14},{18,16},{20... | collective-permute-start | bytes 98312 | tf_op jit(solution)/shard_map/ppermute | solution.py:19
  37.7 4.4 %gather_fusion.3 = bf16[512,2,512]{2,0,1:T(8,128)(2,1)S(1)} fusion(bf16[2,128,512]{2,1,0:T(8,128)(2,1)S(1)} %copy-done.1, s32[1024]{0:T(1024)S(1)} %get-tuple-element.39), kind=kCustom, calls=%fused_computation.2.clone | custom fusion | bytes 2099200 | tf_op jit(solution)/shard_map/jit(_take)/gather | solution.py:82
  42.2 2.4 %all-gather.1 = bf16[1,512,512]{2,1,0:T(8,128)(2,1)} all-gather(bf16[1,512,256]{2,1,0:T(8,128)(2,1)S(1)} %get-tuple-element.16), channel_id=3, replica_groups=mesh['dom'=16,'mem'=2] {'mem'}, dimensions={2}, use_global_device_ids=true | all-gather | bytes 786432 | tf_op jit(solution)/shard_map/all_gather | solution.py:66
  44.7 2.3 %all-gather.3 = bf16[1,512,512]{2,1,0:T(8,128)(2,1)} all-gather(bf16[1,512,256]{2,1,0:T(8,128)(2,1)S(1)} %get-tuple-element.17), channel_id=5, replica_groups=mesh['dom'=16,'mem'=2] {'mem'}, dimensions={2}, use_global_device_ids=true | all-gather | bytes 786432 | tf_op jit(solution)/shard_map/all_gather | solution.py:68
  47.1 2.3 %all-gather.5 = bf16[1,512,512]{2,1,0:T(8,128)(2,1)} all-gather(bf16[1,512,256]{2,1,0:T(8,128)(2,1)S(1)} %get-tuple-element.15), channel_id=7, replica_groups=mesh['dom'=16,'mem'=2] {'mem'}, dimensions={2}, use_global_device_ids=true | all-gather | bytes 786432 | tf_op jit(solution)/shard_map/all_gather | solution.py:66
  49.4 2.6 %all-gather.7 = bf16[1,512,512]{2,1,0:T(8,128)(2,1)} all-gather(bf16[1,512,256]{2,1,0:T(8,128)(2,1)S(1)} %get-tuple-element.18), channel_id=9, replica_groups=mesh['dom'=16,'mem'=2] {'mem'}, dimensions={2}, use_global_device_ids=true | all-gather | bytes 786432 | tf_op jit(solution)/shard_map/all_gather | solution.py:68
  52.0 5.0 %fusion.29 = bf16[2,512,512]{2,0,1:T(2,128)(2,1)} fusion(bf16[512,2,512]{2,0,1:T(8,128)(2,1)S(1)} %gather_fusion.3, pred[512]{0:T(512)(128)(4,1)S(1)} %compare_and_fusion), kind=kLoop, calls=%fused_computation.45 | loop fusion | flops 524288 | bytes 2097664 | tf_op jit(solution)/shard_map/jit(_take)/select_n | solution.py:82
  61.0 3.6 %gather_fusion.2 = bf16[512,2,512]{2,1,0:T(2,128)(2,1)S(1)} fusion(bf16[2,192,512]{2,0,1:T(2,128)(2,1)S(1)} %pad_maximum_fusion.5, s32[1024]{0:T(1024)S(1)} %pad_clamp_fusion.1), kind=kCustom, calls=%fused_computation.1.clone | custom fusion | bytes 2099200 | tf_op jit(solution)/shard_map/jit(_take)/gather | solution.py:81
  66.5 3.3 %pad_maximum_fusion = bf16[2,512,1536]{2,0,1:T(2,128)(2,1)S(1)} fusion(bf16[2,512,512]{2,0,1:T(2,128)(2,1)S(1)} %copy-done.4, bf16[2,512,512]{2,0,1:T(2,128)(2,1)S(1)} %fusion.27, bf16[2,512,512]{2,0,1:T(2,128)(2,1)S(1)} %copy-done.6), kind=kLoop, calls=%fused_computation.8 | loop fusion | flops 9437184 | bytes 6291456 | tf_op jit(solution)/shard_map/concatenate | solution.py:83
  69.8 2.1 %copy.63 = bf16[2,512,1536]{2,1,0:T(8,128)(2,1)} copy(bf16[2,512,1536]{2,0,1:T(2,128)(2,1)S(1)} %pad_maximum_fusion) | data formatting | bytes 6291456 | tf_op jit(solution)/shard_map/concatenate | solution.py:83
  72.0 5.0 %fusion.70 = (f32[1024]{0:T(1024)S(1)}, f32[1024,512]{1,0:T(8,128)S(1)}) fusion(bf16[1,512,512]{2,1,0:T(8,128)(2,1)} %all-gather.1, bf16[1024,1536]{1,0:T(8,128)(2,1)} %bitcast.238, bf16[1,1536,512]{2,1,0:T(8,128)(2,1)} %all-gather.13.cloned.1.call-done), kind=kOutput, calls=%fused_computation.179 | convolution fusion | flops 2150628352 | bytes 7344128 | tf_op jit(solution)/shard_map/dot_general | solution.py:28
  77.8 5.5 %fusion.3 = bf16[2,512,512]{2,0,1:T(2,128)(2,1)S(1)} fusion(f32[2,512,512]{2,1,0:T(8,128)S(1)} %bitcast.237, pred[512]{0:T(512)(128)(4,1)S(1)} %iota_compare_fusion.1, bf16[2,512,512]{2,1,0:T(8,128)(2,1)S(1)} %copy-done.2), kind=kLoop, calls=%fused_computation.15 | loop fusion | flops 2097152 | bytes 4194816 | tf_op jit(solution)/shard_map/convert_element_type | solution.py:93
  88.9 3.6 %gather_fusion.7 = bf16[512,2,512]{2,1,0:T(2,128)(2,1)S(1)} fusion(bf16[2,128,512]{2,0,1:T(2,128)(2,1)S(1)} %copy.69, s32[1024]{0:T(1024)S(1)} %get-tuple-element.39), kind=kCustom, calls=%fused_computation.7.clone | custom fusion | bytes 2099200 | tf_op jit(solution)/shard_map/jit(_take)/gather | solution.py:82
  102.1 3.7 %all-to-all-start.1 = ((bf16[16,2,2,512]{3,1,2,0:T(2,128)(2,1)}), bf16[16,2,2,512]{3,1,2,0:T(2,128)(2,1)S(1)}, u32[]{:S(2)}, u32[]{:S(2)}) async-start(bf16[16,2,2,512]{3,1,2,0:T(2,128)(2,1)} %constant_dynamic-update-slice_fusion.16), calls=%async_computation.1 | async-start | bytes 131072 | tf_op jit(solution)/shard_map/all_to_all | solution.py:77
  108.8 3.7 %collective-permute-start.3 = (bf16[2,16,512]{1,2,0:T(8,128)(2,1)S(1)}, bf16[2,16,512]{1,2,0:T(8,128)(2,1)}, u32[]{:S(2)}, u32[]{:S(2)}) collective-permute-start(bf16[2,16,512]{1,2,0:T(8,128)(2,1)S(1)} %get-tuple-element.20), channel_id=1, source_target_pairs={{2,0},{4,2},{6,4},{8,6},{10,8},{12,10},{14,12},{16,14},{18,16},{20... | collective-permute-start | bytes 98312 | tf_op jit(solution)/shard_map/ppermute | solution.py:19
  112.5 2.6 %fusion.30 = bf16[2,512,512]{2,0,1:T(2,128)(2,1)} fusion(bf16[512,2,512]{2,1,0:T(2,128)(2,1)S(1)} %gather_fusion.7, pred[512]{0:T(512)(128)(4,1)S(1)} %compare_and_fusion), kind=kLoop, calls=%fused_computation.46 | loop fusion | flops 524288 | bytes 2097664 | tf_op jit(solution)/shard_map/jit(_take)/select_n | solution.py:82
  115.3 5.0 %collective-permute-done.2 = bf16[2,16,512]{1,2,0:T(8,128)(2,1)S(1)} collective-permute-done((bf16[2,16,512]{1,2,0:T(8,128)(2,1)}, bf16[2,16,512]{1,2,0:T(8,128)(2,1)S(1)}, u32[]{:S(2)}, u32[]{:S(2)}) %collective-permute-start.2) | collective-permute-done | bytes 32800 | tf_op jit(solution)/shard_map/ppermute | solution.py:16
  124.0 3.6 %gather_fusion.6 = bf16[512,2,512]{2,1,0:T(2,128)(2,1)S(1)} fusion(bf16[2,192,512]{2,0,1:T(2,128)(2,1)S(1)} %copy.73, s32[1024]{0:T(1024)S(1)} %pad_clamp_fusion.1), kind=kCustom, calls=%fused_computation.6.clone | custom fusion | bytes 2099200 | tf_op jit(solution)/shard_map/jit(_take)/gather | solution.py:81
  129.5 3.3 %pad_maximum_fusion.1 = bf16[2,512,1536]{2,0,1:T(2,128)(2,1)S(1)} fusion(bf16[2,512,512]{2,0,1:T(2,128)(2,1)S(1)} %copy-done.5, bf16[2,512,512]{2,0,1:T(2,128)(2,1)S(1)} %fusion.28, bf16[2,512,512]{2,0,1:T(2,128)(2,1)S(1)} %fusion.3), kind=kLoop, calls=%fused_computation.9 | loop fusion | flops 9437184 | bytes 6291456 | tf_op jit(solution)/shard_map/concatenate | solution.py:83
  132.8 2.1 %copy.75 = bf16[2,512,1536]{2,1,0:T(8,128)(2,1)} copy(bf16[2,512,1536]{2,0,1:T(2,128)(2,1)S(1)} %pad_maximum_fusion.1) | data formatting | bytes 6291456 | tf_op jit(solution)/shard_map/concatenate | solution.py:83
  134.9 5.0 %fusion.76 = (f32[1024]{0:T(1024)S(1)}, f32[1024,512]{1,0:T(8,128)S(1)}) fusion(bf16[1,512,512]{2,1,0:T(8,128)(2,1)} %all-gather.5, bf16[1024,1536]{1,0:T(8,128)(2,1)} %bitcast.239, bf16[1,1536,512]{2,1,0:T(8,128)(2,1)} %all-gather.17.cloned.1.call-done), kind=kOutput, calls=%fused_computation.181 | convolution fusion | flops 2150628352 | bytes 7344128 | tf_op jit(solution)/shard_map/dot_general | solution.py:28
  140.8 4.3 %fusion.1 = bf16[2,512,512]{2,0,1:T(2,128)(2,1)S(1)} fusion(f32[2,512,512]{2,1,0:T(8,128)S(1)} %bitcast.236, bf16[2,512,512]{2,0,1:T(2,128)(2,1)S(1)} %fusion.3, pred[512]{0:T(512)(128)(4,1)S(1)} %iota_compare_fusion.1), kind=kLoop, calls=%fused_computation.12 | loop fusion | flops 2097152 | bytes 4194816 | tf_op jit(solution)/shard_map/convert_element_type | solution.py:93
  (169 shorter events, 51.4 us)
Async XLA Ops:
  7.2 4.8 %copy-start = (s32[16,16,2]{1,2,0:T(2,128)S(1)}, s32[16,16,2]{1,2,0:T(2,128)}, u32[]{:S(2)}) copy-start(s32[16,16,2]{1,2,0:T(2,128)} %param.27) | copy-start | bytes 6148
  7.2 2.9 %copy-start.9 = (bf16[2,1024,256]{2,1,0:T(8,128)(2,1)S(1)}, bf16[2,1024,256]{2,1,0:T(8,128)(2,1)}, u32[]{:S(2)}) copy-start(bf16[2,1024,256]{2,1,0:T(8,128)(2,1)} %param.30) | copy-start | bytes 3145732
  7.2 64.8 %all-gather.13.cloned.1.call-start = ((), (), s32[]{:S(2)}) async-start(), calls=%async_computation.2 | async-start | bytes 2359296 | tf_op jit(solution)/shard_map/all_gather | solution.py:65
  10.0 2.2 %copy-start.1 = (bf16[2,128,512]{2,1,0:T(8,128)(2,1)S(1)}, bf16[2,128,512]{2,1,0:T(8,128)(2,1)}, u32[]{:S(2)}) copy-start(bf16[2,128,512]{2,1,0:T(8,128)(2,1)} %param.21) | copy-start | bytes 786436
  10.0 21.0 %copy-start.20 = (s32[32]{0:T(128)S(1)}, s32[32]{0:T(128)}, u32[]{:S(2)}) copy-start(s32[32]{0:T(128)} %param.26) | copy-start | bytes 388
  10.0 74.1 %all-gather.15.cloned.1.call-start = ((), (), s32[]{:S(2)}) async-start(), calls=%async_computation.3 | async-start | bytes 1572864 | tf_op jit(solution)/shard_map/all_gather | solution.py:67
  11.2 26.4 %copy-start.15 = (s32[512]{0:T(512)S(1)}, s32[512]{0:T(512)}, u32[]{:S(2)}) copy-start(s32[512]{0:T(512)} %param.23) | copy-start | bytes 6148
  11.2 123.8 %all-gather.17.cloned.1.call-start = ((), (), s32[]{:S(2)}) async-start(), calls=%async_computation.4 | async-start | bytes 2359296 | tf_op jit(solution)/shard_map/all_gather | solution.py:65
  22.6 37.7 %all-to-all-start = ((bf16[16,2,2,512]{3,2,1,0:T(2,128)(2,1)}), bf16[16,2,2,512]{3,2,1,0:T(2,128)(2,1)S(1)}, u32[]{:S(2)}, u32[]{:S(2)}) async-start(bf16[16,2,2,512]{3,2,1,0:T(2,128)(2,1)} %constant_dynamic-update-slice_fusion), calls=%async_computation | async-start | bytes 131072 | tf_op jit(solution)/shard_map/all_to_all | solution.py:77
  30.9 115.1 %all-gather.19.cloned.1.call-start = ((), (), s32[]{:S(2)}) async-start(), calls=%async_computation.5 | async-start | bytes 1572864 | tf_op jit(solution)/shard_map/all_gather | solution.py:67
  31.9 28.3 %collective-permute-start = (bf16[2,16,512]{2,1,0:T(8,128)(2,1)S(1)}, bf16[2,16,512]{2,1,0:T(8,128)(2,1)S(1)}, u32[]{:S(2)}, u32[]{:S(2)}) collective-permute-start(bf16[2,16,512]{2,1,0:T(8,128)(2,1)S(1)} %get-tuple-element.21), channel_id=1, source_target_pairs={{0,2},{2,4},{4,6},{6,8},{8,10},{10,12},{12,14},{14,16},{16,18},{18... | collective-permute-start | bytes 98312 | tf_op jit(solution)/shard_map/ppermute | solution.py:16
  33.9 26.4 %collective-permute-start.1 = (bf16[2,16,512]{2,1,0:T(8,128)(2,1)S(1)}, bf16[2,16,512]{2,1,0:T(8,128)(2,1)S(1)}, u32[]{:S(2)}, u32[]{:S(2)}) collective-permute-start(bf16[2,16,512]{2,1,0:T(8,128)(2,1)S(1)} %get-tuple-element.22), channel_id=1, source_target_pairs={{2,0},{4,2},{6,4},{8,6},{10,8},{12,10},{14,12},{16,14},{18,16},{20... | collective-permute-start | bytes 98312 | tf_op jit(solution)/shard_map/ppermute | solution.py:19
  37.6 4.5 %copy-start.12 = (bf16[2,512,256]{2,1,0:T(8,128)(2,1)S(1)}, bf16[2,512,256]{2,1,0:T(8,128)(2,1)}, u32[]{:S(2)}) copy-start(bf16[2,512,256]{2,1,0:T(8,128)(2,1)} %param.29) | copy-start | bytes 1572868
  37.6 7.0 %copy-start.16 = (f32[2,512]{1,0:T(2,128)S(1)}, f32[2,512]{1,0:T(2,128)}, u32[]{:S(2)}) copy-start(f32[2,512]{1,0:T(2,128)} %param.32) | copy-start | bytes 12292
  37.7 7.0 %copy-start.17 = (f32[2,512]{1,0:T(2,128)S(1)}, f32[2,512]{1,0:T(2,128)}, u32[]{:S(2)}) copy-start(f32[2,512]{1,0:T(2,128)} %param.33) | copy-start | bytes 12292
  42.1 2.6 %copy-start.13 = (bf16[2,512,256]{2,1,0:T(8,128)(2,1)S(1)}, bf16[2,512,256]{2,1,0:T(8,128)(2,1)}, u32[]{:S(2)}) copy-start(bf16[2,512,256]{2,1,0:T(8,128)(2,1)} %param.31) | copy-start | bytes 1572868
  42.1 4.9 %copy-start.18 = (f32[2,512]{1,0:T(2,128)S(1)}, f32[2,512]{1,0:T(2,128)}, u32[]{:S(2)}) copy-start(f32[2,512]{1,0:T(2,128)} %param.34) | copy-start | bytes 12292
  42.2 4.9 %copy-start.19 = (f32[2,512]{1,0:T(2,128)S(1)}, f32[2,512]{1,0:T(2,128)}, u32[]{:S(2)}) copy-start(f32[2,512]{1,0:T(2,128)} %param.35) | copy-start | bytes 12292
  49.4 8.7 %copy-start.2 = (bf16[2,512,512]{2,1,0:T(8,128)(2,1)S(1)}, bf16[2,512,512]{2,1,0:T(8,128)(2,1)}, u32[]{:S(2)}) copy-start(bf16[2,512,512]{2,1,0:T(8,128)(2,1)} %param.22) | copy-start | bytes 3145732
  58.1 25.7 %copy-start.7 = (bf16[2,128,512]{1,2,0:T(8,128)(2,1)}, bf16[2,128,512]{1,2,0:T(8,128)(2,1)S(1)}, u32[]{:S(2)}) copy-start(bf16[2,128,512]{1,2,0:T(8,128)(2,1)S(1)} %copy.54) | copy-start | bytes 786436
  102.1 13.0 %all-to-all-start.1 = ((bf16[16,2,2,512]{3,1,2,0:T(2,128)(2,1)}), bf16[16,2,2,512]{3,1,2,0:T(2,128)(2,1)S(1)}, u32[]{:S(2)}, u32[]{:S(2)}) async-start(bf16[16,2,2,512]{3,1,2,0:T(2,128)(2,1)} %constant_dynamic-update-slice_fusion.16), calls=%async_computation.1 | async-start | bytes 131072 | tf_op jit(solution)/shard_map/all_to_all | solution.py:77
  106.9 13.4 %collective-permute-start.2 = (bf16[2,16,512]{1,2,0:T(8,128)(2,1)}, bf16[2,16,512]{1,2,0:T(8,128)(2,1)S(1)}, u32[]{:S(2)}, u32[]{:S(2)}) collective-permute-start(bf16[2,16,512]{1,2,0:T(8,128)(2,1)} %get-tuple-element.19), channel_id=1, source_target_pairs={{0,2},{2,4},{4,6},{6,8},{8,10},{10,12},{12,14},{14,16},{16,18},{18... | collective-permute-start | bytes 98312 | tf_op jit(solution)/shard_map/ppermute | solution.py:16
  108.8 13.4 %collective-permute-start.3 = (bf16[2,16,512]{1,2,0:T(8,128)(2,1)S(1)}, bf16[2,16,512]{1,2,0:T(8,128)(2,1)}, u32[]{:S(2)}, u32[]{:S(2)}) collective-permute-start(bf16[2,16,512]{1,2,0:T(8,128)(2,1)S(1)} %get-tuple-element.20), channel_id=1, source_target_pairs={{2,0},{4,2},{6,4},{8,6},{10,8},{12,10},{14,12},{16,14},{18,16},{20... | collective-permute-start | bytes 98312 | tf_op jit(solution)/shard_map/ppermute | solution.py:19
  145.2 3.5 %copy-start.3 = (bf16[2,512,512]{2,1,0:T(8,128)(2,1)}, bf16[2,512,512]{2,1,0:T(8,128)(2,1)S(1)}, u32[]{:S(2)}) copy-start(bf16[2,512,512]{2,1,0:T(8,128)(2,1)S(1)} %copy.81) | copy-start | bytes 3145732
  (7 other events, 11.6 us)
Sparse Core Ops, SparseCore 0:
  10.1 12.1 all-gather.12
  23.9 9.9 all-gather.14
  35.4 10.6 all-gather.16
  47.5 10.3 all-gather.18
